TPU v7x, 32 devices: a whole 2x2x4 slice. The times are simulated.
32 devices in a mesh: aux: 4 (over y, x), pair: 8 (over z, core).
Axes of the slice: x: 2, y: 2, z: 4, core: 2. Of those that a mesh axis runs over, the one named last changes fastest.
Arguments:
- m_panels: bfloat16 [40000, 8192], P('aux', 'pair'), may hold values from -6 to 6
- lower_cols: bfloat16 [2, 512, 40000], P(None, 'pair', 'aux'), may hold values from -0.2 to 0.2, as said below
- diag_inverses: float32 [2, 512, 512], replicated, may hold values from -0.2 to 2, as said below
Outputs:
- remainder: bfloat16 [40000, 8192], P('aux', 'pair')
- solved: bfloat16 [2, 512, 8192], P(None, None, 'pair')
Inputs may be any that keep to these rules, and one draw needn't show every extreme that they name: lower_cols[k] is zero in the pivot rows of panels 0 to k (the factor is lower triangular and its diagonal blocks are given by their inverses). Each diag_inverses[k] is lower triangular.
All inputs are finite; a program needn't handle non-finite values.
Results may differ from a plain program's by a relative error of at most 0.0047.
Values may be sent and summed in bfloat16 or wider, within the bound.
A program may use at most 192 MiB of HBM per device.

v0:
```python
import jax
import jax.numpy as jnp
from jax import lax
from jax.sharding import PartitionSpec as P


def spread(block, axis, source):
    block = jnp.where(lax.axis_index(axis) == source, block, jnp.zeros_like(block))
    return lax.psum(block, axis)


def settle(panel, pivot, diag_inverses):
    local = jnp.dot(
        diag_inverses[panel],
        pivot,
        precision=lax.Precision.HIGHEST,
        preferred_element_type=jnp.float32,
    ).astype(jnp.bfloat16)
    return spread(local, "aux", panel)


def shards(m_panels, lower_cols, diag_inverses):
    panels = diag_inverses.shape[0]
    width = diag_inverses.shape[1]
    work = m_panels.astype(jnp.float32)
    results = []
    for panel in range(panels):
        solved_rows = settle(panel, work[:width], diag_inverses)

        def subtract(carry, piece, start, solved_rows=solved_rows):
            return carry - lax.dot_general(
                piece, solved_rows, (((0,), (0,)), ((), ())), preferred_element_type=jnp.float32
            )

        work = subtract(
            work, lax.all_gather(lower_cols[panel], "pair", axis=0, tiled=True), jnp.int32(0)
        )
        results.append(solved_rows)
    return (work.astype(jnp.bfloat16), jnp.stack(results))


def solution(mesh):
    placed = (P("aux", "pair"), P(None, "pair", "aux"), P())
    return jax.shard_map(
        shards,
        mesh=mesh,
        in_specs=placed,
        out_specs=(P("aux", "pair"), P(None, None, "pair")),
        check_vma=False,
    )
```

profile of v0, /device:TPU:0, one launch (start us, length us, event | category | flops | bytes accessed | tf_op | source)
XLA Modules:
  0.0 282.0 jit_solution(16829166616042446684)
XLA Ops:
  8.0 0.0 all-reduce.3.cloned.1.call-start
  8.0 4.3 %fusion.8 = bf16[512,1024]{1,0:T(8,128)(2,1)} fusion(bf16[10000,1024]{1,0:T(8,128)(2,1)} %param.3, f32[2,512,512]{2,1,0:T(8,128)} %param.5, pred[]{:T(512)S(6)} %eq.6), kind=kOutput, calls=%fused_computation.10 | convolution fusion | flops 3222274048 | bytes 3145729 | tf_op jit(solution)/shard_map/dot_general | solution.py:13
  12.4 0.0 all-reduce.3.cloned.1.call-update
  12.4 0.0 all-gather.5.cloned.1.call-start
  12.4 3.3 %fusion.20 = (bf16[1,64,10000]{2,1,0:T(8,128)(2,1)}, bf16[1,64,10000]{2,1,0:T(8,128)(2,1)}) fusion(bf16[2,64,10000]{2,1,0:T(8,128)(2,1)} %param.4), kind=kLoop, calls=%fused_computation.18 | loop fusion | bytes 5120000 | tf_op jit(solution)/shard_map/slice | solution.py:36
  15.8 0.0 all-gather.5.cloned.1.call-update
  15.8 0.0 all-reduce.5.cloned.1.call-start
  15.9 0.0 copy-start.1
  15.9 51.9 %all-reduce.3.cloned.1.call-done = bf16[512,1024]{1,0:T(8,128)(2,1)} async-done(((bf16[512,1024]{1,0:T(8,128)(2,1)}), bf16[512,1024]{1,0:T(8,128)(2,1)}) %all-reduce.3.cloned.1.call-update) | async-done | bytes 1048592 | tf_op jit(solution)/shard_map/psum | solution.py:9
  67.7 0.0 copy-start
  67.7 49.1 %all-gather.5.cloned.1.call-done = bf16[1,512,10000]{2,1,0:T(8,128)(2,1)} async-done(((bf16[1,64,10000]{2,1,0:T(8,128)(2,1)}), bf16[1,512,10000]{2,1,0:T(8,128)(2,1)}) %all-gather.5.cloned.1.call-update) | async-done | bytes 10240016 | tf_op jit(solution)/shard_map/all_gather | solution.py:36
  116.8 27.4 %bitcast_subtract_fusion.1 = f32[10000,1024]{1,0:T(8,128)} fusion(bf16[10000,1024]{1,0:T(8,128)(2,1)} %param.3, bf16[512,1024]{1,0:T(8,128)(2,1)} %all-reduce.3.cloned.1.call-done, bf16[1,512,10000]{2,1,0:T(8,128)(2,1)} %all-gather.5.cloned.1.call-done), kind=kOutput, calls=%fused_computation.2 | convolution fusion | flops 10506240000 | bytes 72728576 | tf_op jit(solution)/shard_map/dot_general | solution.py:31
  144.2 0.0 copy-done.1
  144.2 6.1 %fusion.12 = bf16[512,1024]{1,0:T(8,128)(2,1)} fusion(f32[10000,1024]{1,0:T(8,128)} %bitcast_subtract_fusion.1, f32[2,512,512]{2,1,0:T(8,128)S(1)} %copy-done.1, pred[]{:T(512)S(6)} %eq.7), kind=kOutput, calls=%fused_computation.12 | convolution fusion | flops 3222274048 | bytes 4194305 | tf_op jit(solution)/shard_map/dot_general | solution.py:13
  150.3 0.0 all-reduce.5.cloned.1.call-update
  150.3 0.2 all-gather.7.cloned.1.call-start
  150.5 0.4 all-gather.7.cloned.1.call-update
  150.9 50.4 %all-reduce.5.cloned.1.call-done = bf16[512,1024]{1,0:T(8,128)(2,1)} async-done(((bf16[512,1024]{1,0:T(8,128)(2,1)}), bf16[512,1024]{1,0:T(8,128)(2,1)}) %all-reduce.5.cloned.1.call-update) | async-done | bytes 1048592 | tf_op jit(solution)/shard_map/psum | solution.py:9
  201.2 0.0 copy-done
  201.2 2.7 pad_maximum_fusion
  204.0 45.5 %all-gather.7.cloned.1.call-done = bf16[1,512,10000]{2,1,0:T(8,128)(2,1)} async-done(((bf16[1,64,10000]{2,1,0:T(8,128)(2,1)}), bf16[1,512,10000]{2,1,0:T(8,128)(2,1)}) %all-gather.7.cloned.1.call-update) | async-done | bytes 10240016 | tf_op jit(solution)/shard_map/all_gather | solution.py:36
  249.5 25.0 %fusion = bf16[10000,1024]{1,0:T(8,128)(2,1)} fusion(f32[10000,1024]{1,0:T(8,128)} %bitcast_subtract_fusion.1, bf16[512,1024]{1,0:T(8,128)(2,1)} %all-reduce.5.cloned.1.call-done, bf16[1,512,10000]{2,1,0:T(8,128)(2,1)} %all-gather.7.cloned.1.call-done), kind=kOutput, calls=%fused_computation.1 | convolution fusion | flops 10506240000 | bytes 72728576 | tf_op jit(solution)/shard_map/dot_general | solution.py:31
Async XLA Ops:
  8.0 59.7 %all-reduce.3.cloned.1.call-start = ((), (), s32[]{:S(2)}) async-start(), calls=%async_computation | async-start | bytes 2097152 | tf_op jit(solution)/shard_map/psum | solution.py:9
  12.4 104.4 %all-gather.5.cloned.1.call-start = ((), (), s32[]{:S(2)}) async-start(), calls=%async_computation.2 | async-start | bytes 11649024 | tf_op jit(solution)/shard_map/all_gather | solution.py:36
  15.8 185.4 %all-reduce.5.cloned.1.call-start = ((), (), s32[]{:S(2)}) async-start(), calls=%async_computation.1 | async-start | bytes 2097152 | tf_op jit(solution)/shard_map/psum | solution.py:9
  15.9 128.3 %copy-start.1 = (f32[2,512,512]{2,1,0:T(8,128)S(1)}, f32[2,512,512]{2,1,0:T(8,128)}, u32[]{:S(2)}) copy-start(f32[2,512,512]{2,1,0:T(8,128)} %param.5) | copy-start | bytes 6291460
  67.7 133.5 %copy-start = (bf16[512,1024]{1,0:T(8,128)(2,1)S(1)}, bf16[512,1024]{1,0:T(8,128)(2,1)}, u32[]{:S(2)}) copy-start(bf16[512,1024]{1,0:T(8,128)(2,1)} %all-reduce.3.cloned.1.call-done) | copy-start | bytes 3145732
  150.3 99.2 %all-gather.7.cloned.1.call-start = ((), (), s32[]{:S(2)}) async-start(), calls=%async_computation.3 | async-start | bytes 11649024 | tf_op jit(solution)/shard_map/all_gather | solution.py:36
Sparse Core Ops, SparseCore 0:
  12.5 55.1 all-reduce.2
  150.4 50.7 all-reduce.4
Sparse Core Ops, SparseCore 1:
  15.9 100.9 all-gather.4
  153.0 96.5 all-gather.6
where the time goes:
time: 282 us
  waiting for transfers between devices  197 us (70%)
  matrix products  62.8 us (22%)
  between operations  15.5 us (5%)
  local copies, waits for them, and re-layouts  3.36 us (1%)
    psum x2, waiting for transfers between devices, spread(): return lax.psum(block, axis)  102 us
    all_gather x2, waiting for transfers between devices, shards(): lax.all_gather(lower_cols[panel], 'pair', axis=0, tiled=True)  94.6 us
    dot_general x2, matrix products, subtract(): lax.dot_general(piece, solved_rows, (((0,), (0,)), ((), ())), preferred_e...  52.4 us
    dot_general x2, matrix products, settle(): jnp.dot(diag_inverses[panel], pivot, precision=lax.Precision.HIGHEST, pre...  10.4 us
  transfers between devices with their start and end apart: 4, of which 4 were waited for; matrix products, arithmetic and copies ran while one was open for 2% of the time, Pallas kernels for 0%

commit v1 on v0

v1 whole, which is shorter than its diff:
```python
import functools

import jax
import jax.numpy as jnp
from jax import lax
from jax.experimental import pallas as pl
from jax.experimental.pallas import tpu as pltpu
from jax.sharding import PartitionSpec as P

CHUNKS = 10
TILE = 256
CORES = 2
CONTRACT = (((0,), (0,)), ((), ()))
MESH = pl.DeviceIdType.MESH


def kernel(aux, chips, chunks, chunk, m_hbm, l_hbm, l_tail, dinv_ref, mbuf, solved_ref,
           lbuf, sbuf, load_sem, ring_sem, swap_sem, left_sem, right_sem, part_sem,
           srecv_sem, ssend_sem):
    rows, columns = m_hbm.shape
    panels, width = dinv_ref.shape[:2]
    even = rows - rows % TILE
    padded = lbuf.shape[-1]
    a = lax.axis_index("aux")
    me = lax.axis_index("pair")
    z, c = me // CORES, lax.rem(me, CORES)
    to_left = {"pair": lax.rem(z + chips - 1, chips) * CORES + c}
    to_right = {"pair": lax.rem(z + 1, chips) * CORES + c}
    partner = {"pair": z * CORES + 1 - c}

    own_load = pltpu.make_async_copy(
        l_hbm.at[:, :, pl.ds(0, even)], lbuf.at[me, :, :, pl.ds(0, even)], load_sem.at[0])
    own_tail = pltpu.make_async_copy(
        l_tail, lbuf.at[me, :, :, pl.ds(even, padded - even)], load_sem.at[3])
    pivot_load = pltpu.make_async_copy(
        m_hbm.at[pl.ds(0, width)], mbuf.at[pl.ds(0, width)], load_sem.at[1])
    rest_load = pltpu.make_async_copy(
        m_hbm.at[pl.ds(width, rows - width)], mbuf.at[pl.ds(width, rows - width)], load_sem.at[2])
    own_load.start()
    own_tail.start()
    pivot_load.start()

    barrier = pltpu.get_barrier_semaphore()
    for peer in (to_left, to_right, partner):
        pl.semaphore_signal(barrier, inc=1, device_id=peer, device_id_type=MESH)
    for step in range(1, aux):
        peer = {"aux": lax.rem(a + step, aux)}
        pl.semaphore_signal(barrier, inc=1, device_id=peer, device_id_type=MESH)
    pl.semaphore_wait(barrier, 2 + aux)
    own_load.wait()
    own_tail.wait()
    rest_load.start()

    def piece(block, j):
        return lbuf.at[block, :, :, pl.ds(pl.multiple_of(j * chunk, 128), chunk)]

    def ring(zb, j, send, peer):
        ref = piece(zb * CORES + c, j)
        return pltpu.make_async_remote_copy(
            src_ref=ref, dst_ref=ref, send_sem=send.at[zb, j], recv_sem=ring_sem.at[zb, j],
            device_id=peer, device_id_type=MESH)

    def swap(zb, j, core):
        ref = piece(zb * CORES + core, j)
        return pltpu.make_async_remote_copy(
            src_ref=ref, dst_ref=ref, send_sem=part_sem.at[zb, j], recv_sem=swap_sem.at[zb, j],
            device_id=partner, device_id_type=MESH)

    def solve(panel):
        def columns_of(i, _):
            cols = pl.ds(pl.multiple_of(i * TILE, TILE), TILE)
            pivot = mbuf[pl.ds(0, width), cols].astype(jnp.float32)
            for before in range(panel):
                factor = lbuf[:, before, :, pl.ds(0, width)].reshape(-1, width)
                pivot = pivot - lax.dot_general(
                    factor, sbuf[before, :, cols], CONTRACT, preferred_element_type=jnp.float32)
            sbuf[panel, :, cols] = jnp.dot(
                dinv_ref[panel], pivot, precision=lax.Precision.HIGHEST,
                preferred_element_type=jnp.float32).astype(jnp.bfloat16)
            return 0

        lax.fori_loop(0, columns // TILE, columns_of, 0)

    def spread(panel, step):
        return pltpu.make_async_remote_copy(
            src_ref=sbuf.at[panel], dst_ref=sbuf.at[panel],
            send_sem=ssend_sem.at[panel, step], recv_sem=srecv_sem.at[panel],
            device_id={"aux": lax.rem(a + step, aux)}, device_id_type=MESH)

    def settle(panel):
        solve(panel)
        for step in range(1, aux):
            spread(panel, step).start()

    def product(here):
        return sum(
            lax.dot_general(
                lbuf[:, panel, :, here].reshape(-1, TILE), sbuf[panel], CONTRACT,
                preferred_element_type=jnp.float32)
            for panel in range(panels))

    def update(j):
        def tile(i, _):
            here = pl.ds(pl.multiple_of(i * TILE, TILE), TILE)
            mbuf[here] = (mbuf[here].astype(jnp.float32) - product(here)).astype(jnp.bfloat16)
            return 0

        tiles = chunk // TILE
        lax.fori_loop(j * tiles, jnp.minimum((j + 1) * tiles, even // TILE), tile, 0)

    def complete(j):
        for zb in range(chips):
            swap(zb, j, 1 - c).wait_recv()

    def tick(t):
        @pl.when(t < chunks)
        def _():
            @pl.when(z > 0)
            def _():
                ring(z, t, left_sem, to_left).start()

            @pl.when(z < chips - 1)
            def _():
                ring(z, t, right_sem, to_right).start()

            swap(z, t, c).start()

        for step in range(1, chips):
            j = t - step
            live = jnp.logical_and(j >= 0, j < chunks)

            @pl.when(jnp.logical_and(live, z + step < chips))
            def _():
                ring(z + step, j, left_sem, to_left).wait_recv()

                @pl.when(z > 0)
                def _():
                    ring(z + step, j, left_sem, to_left).start()

                swap(z + step, j, c).start()

            @pl.when(jnp.logical_and(live, z >= step))
            def _():
                ring(z - step, j, right_sem, to_right).wait_recv()

                @pl.when(z < chips - 1)
                def _():
                    ring(z - step, j, right_sem, to_right).start()

                swap(z - step, j, c).start()

        j = t - (chips - 1)

        @pl.when(jnp.logical_and(j >= 0, j < chunks))
        def _():
            complete(j)

    first = max(chips + panels, chunks // 2 + chips)
    last = chunks + chips - 1

    def ticks(t, _):
        tick(t)
        return 0

    tick(jnp.int32(0))
    pivot_load.wait()

    @pl.when(a == 0)
    def _():
        settle(0)

    lax.fori_loop(1, chips, ticks, 0)
    for panel in range(1, panels):
        @pl.when(a == panel)
        def _(panel=panel):
            for before in range(panel):
                spread(before, 1).wait_recv()
            settle(panel)

        lax.fori_loop(chips - 1 + panel, chips + panel, ticks, 0)
    lax.fori_loop(chips - 1 + panels, first, ticks, 0)

    for panel in range(panels):
        @pl.when(jnp.logical_and(a != panel, jnp.logical_or(a < panel, a >= panels)))
        def _(panel=panel):
            spread(panel, 1).wait_recv()
    rest_load.wait()
    solved_ref[...] = sbuf[...]

    def updates(j, _):
        update(j)
        return 0

    lax.fori_loop(0, first - chips + 1, updates, 0)

    def both(t, _):
        tick(t)
        update(t - (chips - 1))
        return 0

    lax.fori_loop(first, last, both, 0)

    if even < rows:
        left = rows - even
        here = pl.ds(even, left)
        total = mbuf[here].astype(jnp.float32) - product(pl.ds(even, TILE))[:left]
        mbuf[here] = total.astype(jnp.bfloat16)

    def drain(j, _):
        for zb in range(chips):
            @pl.when(jnp.logical_and(z > 0, z <= zb))
            def _():
                ring(jnp.int32(zb), j, left_sem, to_left).wait_send()

            @pl.when(jnp.logical_and(z < chips - 1, z >= zb))
            def _():
                ring(jnp.int32(zb), j, right_sem, to_right).wait_send()

            swap(jnp.int32(zb), j, c).wait_send()
        return 0

    lax.fori_loop(0, chunks, drain, 0)
    for panel in range(panels):
        @pl.when(a == panel)
        def _(panel=panel):
            for step in range(1, aux):
                spread(panel, step).wait_send()


def shards(aux, pair, m_panels, lower_cols, diag_inverses):
    panels, width = diag_inverses.shape[:2]
    rows, columns = m_panels.shape
    part = lower_cols.shape[1]
    chips = pair // CORES
    chunk = max(-(-rows // (CHUNKS * TILE)), -(-width // TILE)) * TILE
    chunks = -(-rows // chunk)
    padded = chunks * chunk
    even = rows - rows % TILE
    tail = jnp.pad(lower_cols[:, :, even:], ((0, 0), (0, 0), (0, padded - rows)))
    anywhere = pl.BlockSpec(memory_space=pl.ANY)
    vmem = pl.BlockSpec(memory_space=pltpu.VMEM)
    dma = pltpu.SemaphoreType.DMA
    return pl.pallas_call(
        functools.partial(kernel, aux, chips, chunks, chunk),
        in_specs=[anywhere, anywhere, anywhere, vmem],
        out_specs=[vmem, vmem],
        out_shape=[
            pltpu.VMEM((rows, columns), jnp.bfloat16),
            jax.ShapeDtypeStruct((panels, width, columns), jnp.bfloat16),
        ],
        scratch_shapes=[
            pltpu.VMEM((pair, panels, part, padded), jnp.bfloat16),
            pltpu.VMEM((panels, width, columns), jnp.bfloat16),
            dma((4,)),
            dma((chips, chunks)),
            dma((chips, chunks)),
            dma((chips, chunks)),
            dma((chips, chunks)),
            dma((chips, chunks)),
            dma((panels,)),
            dma((panels, aux)),
        ],
        compiler_params=pltpu.CompilerParams(
            collective_id=0, has_side_effects=True, vmem_limit_bytes=40 * 1024 * 1024),
    )(m_panels, lower_cols, tail, diag_inverses)


def solution(mesh):
    placed = (P("aux", "pair"), P(None, "pair", "aux"), P())
    return jax.shard_map(
        functools.partial(shards, mesh.shape["aux"], mesh.shape["pair"]),
        mesh=mesh,
        in_specs=placed,
        out_specs=(P("aux", "pair"), P(None, None, "pair")),
        check_vma=False,
    )
```

time: 282 us -> 195 us (0.69)
  waiting for transfers between devices: 197 us -> 0 us
  Pallas kernels: 0 us -> 184 us
  matrix products: 62.8 us -> 0 us
  between operations: 15.5 us -> 0.65 us
  local copies, waits for them, and re-layouts: 3.36 us -> 10.2 us
    pallas_call x0 -> x1, Pallas kernels: none -> 184 us  [shards(): pl.pallas_call(functools.partial(kernel, aux, chips, chunks, chunk), in_s...]
    psum x2 -> x0, waiting for transfers between devices: 102 us -> none  [spread(): return lax.psum(block, axis)]
    all_gather x2 -> x0, waiting for transfers between devices: 94.6 us -> none  [shards(): lax.all_gather(lower_cols[panel], 'pair', axis=0, tiled=True)]
    dot_general x4 -> x0, matrix products: 62.8 us -> none  [the longest x2 52.4 us: subtract(): lax.dot_general(piece, solved_rows, (((0,), (0,)), ((), ())), preferred_e...]
    unnamed x4, local copies, waits for them, and re-layouts: 0.01 us -> 8.82 us
  transfers between devices with their start and end apart: 4 -> 0, of which waited for: 4 -> 0; matrix products, arithmetic and copies ran while one was open for 2% -> 0% of each run, Pallas kernels for 0% -> 0%
where the time goes in v1:
time: 195 us; the launch traced here: 194 us
  Pallas kernels  184 us (94%)
  local copies, waits for them, and re-layouts  10.2 us (5%)
    pallas_call x1, Pallas kernels, shards(): pl.pallas_call(functools.partial(kernel, aux, chips, chunks, chunk), in_s...  184 us
    unnamed x4, local copies, waits for them, and re-layouts  8.82 us

profile of v1, /device:TPU:0, one launch (start us, length us, event | category | flops | bytes accessed | tf_op | source)
XLA Modules:
  0.0 194.5 jit_solution(16273460914320475264)
XLA Ops:
  0.6 0.8 slice.3
  1.4 0.6 pad.4.l_tail
  2.0 183.6 %shard_map.50 = (bf16[10000,1024]{1,0:T(8,128)(2,1)S(1)}, bf16[2,512,1024]{2,1,0:T(8,128)(2,1)}) custom-call(bf16[10000,1024]{1,0:T(8,128)(2,1)} %m_hbm.1, bf16[2,64,10000]{2,1,0:T(8,128)(2,1)} %l_hbm.1, bf16[2,64,256]{2,1,0:T(8,128)(2,1)} %pad.4.l_tail, f32[2,512,512]{2,1,0:T(8,128)} %dinv_ref.1), custom_call_target="tpu_custom_call" | custom-call | tf_op jit(solution)/shard_map/pallas_call | solution.py:243
  185.7 0.0 copy-start
  185.7 7.5 %copy.7 = bf16[10000,1024]{1,0:T(8,128)(2,1)} copy(bf16[10000,1024]{1,0:T(8,128)(2,1)S(1)} %get-tuple-element.2) | data formatting | bytes 40960000
  193.2 0.0 copy-done
  193.2 1.3 copy.8
Async XLA Ops:
  185.7 7.5 %copy-start = (bf16[2,512,1024]{2,1,0:T(8,128)(2,1)S(1)}, bf16[2,512,1024]{2,1,0:T(8,128)(2,1)}, u32[]{:S(2)}) copy-start(bf16[2,512,1024]{2,1,0:T(8,128)(2,1)} %get-tuple-element.7) | copy-start | bytes 6291460
